TPU v7x, 32 devices: a whole 2x2x4 slice. The times are simulated.
32 devices in a mesh: dp: 4 (over z), ctx: 8 (over y, x, core).
Axes of the slice: x: 2, y: 2, z: 4, core: 2. Of those that a mesh axis runs over, the one named last changes fastest.
Arguments:
- tokens: bfloat16 [4, 4096, 1024], P('dp', 'ctx'), may hold values from -60 to 60
- kept: int32 [4, 2048], P('dp', 'ctx'), may hold values from 0 to 4095, as said below
- gain_attn: float32 [1024], replicated, may hold values from 0.25 to 1.75
- gain_ffn: float32 [1024], replicated, may hold values from 0.25 to 1.75
- w_query: bfloat16 [1024, 512], P(None, 'ctx'), may hold values from -4 to 4
- w_key: bfloat16 [1024, 512], P(None, 'ctx'), may hold values from -4 to 4
- w_value: bfloat16 [1024, 512], P(None, 'ctx'), may hold values from -0.1875 to 0.1875
- w_out: bfloat16 [512, 1024], P('ctx'), may hold values from -0.25 to 0.25
- expert_ids: int32 [4, 2048, 1], P('dp', 'ctx'), may hold values from 0 to 31; in each aligned block of 256 rows (0 to 255, 256 to 511, ..., all dimensions but the last counted through in order) at most 16 rows name the same one
- w_in: bfloat16 [32, 1024, 2816], P(('dp', 'ctx')), may hold values from -0.1875 to 0.1875
- w_back: bfloat16 [32, 2816, 1024], P(('dp', 'ctx')), may hold values from -0.109375 to 0.109375
Outputs:
- blended: bfloat16 [4, 4096, 1024], P('dp', 'ctx')
Inputs may be any that keep to these rules, and one draw needn't show every extreme that they name: `kept`: in each document row, entries j * 256 to (j + 1) * 256 - 1 are strictly increasing positions from j * 512 to (j + 1) * 512 - 1. `expert_ids`: in each aligned block of 256 rows (the kept positions of one block b) no expert is named more than 16 times.
All inputs are finite; a program needn't handle non-finite values.
Results may differ from a plain program's by a relative error of at most 0.007.
Values may be sent and summed in bfloat16 or wider, within the bound.
A program may use at most 64 MiB of HBM per device.

v0:
```python
import math

import jax
import jax.numpy as jnp
from jax import lax
from jax.sharding import PartitionSpec as P

HS = 64


eps_norm = 1e-06
score_gain = 2.5


def rms_scale(values, gain):
    values = values.astype(jnp.float32)
    power = jnp.mean(values * values, axis=-1, keepdims=True)
    return values * lax.rsqrt(power + eps_norm) * gain


def attend(queries, keys, values):
    count, heads_here, width = queries.shape
    block = 512
    scale = score_gain / math.sqrt(width)
    blocks = queries.reshape(count // block, block, heads_here, width)

    def one_block(block_rows):
        scores = (
            jnp.einsum("qhd,khd->hqk", block_rows, keys, preferred_element_type=jnp.float32) * scale
        )
        top = jnp.max(scores, axis=-1, keepdims=True)
        weights = jnp.exp(scores - top)
        probs = (weights / jnp.sum(weights, axis=-1, keepdims=True)).astype(jnp.bfloat16)
        mixed = jnp.einsum("hqk,khd->qhd", probs, values, preferred_element_type=jnp.float32)
        return mixed.astype(jnp.bfloat16)

    return lax.map(one_block, blocks).reshape(count, heads_here, width)


def body(
    tokens, kept, gain_attn, gain_ffn, w_query, w_key, w_value, w_out, expert_ids, w_in, w_back
):
    document = tokens[0]
    shard_len, width_model = document.shape
    ctx_count = lax.axis_size("ctx")
    dp_count = lax.axis_size("dp")
    local = kept[0] - lax.axis_index("ctx") * shard_len
    rows = jnp.take(document, local, axis=0)
    keep_here = rows.shape[0]
    normed = rms_scale(rows, gain_attn).astype(jnp.bfloat16)
    head_width = HS
    heads_here = w_query.shape[1] // head_width
    stacked = jnp.stack([w_query, w_key, w_value], axis=1)
    triple = jnp.einsum(
        "td,dcf->tcf",
        normed,
        lax.all_gather(stacked, "ctx", axis=2, tiled=True),
        preferred_element_type=jnp.float32,
    ).astype(jnp.bfloat16)
    triple = triple.reshape(keep_here, 3, heads_here * ctx_count, head_width)
    gathered = lax.all_to_all(triple, "ctx", split_axis=2, concat_axis=0, tiled=True)
    mixed = attend(gathered[:, 0], gathered[:, 1], gathered[:, 2])
    returned = lax.all_to_all(mixed, "ctx", split_axis=0, concat_axis=1, tiled=True)
    flat_back = returned.reshape(keep_here, heads_here * ctx_count * head_width)
    attn = jnp.dot(
        flat_back,
        lax.all_gather(w_out, "ctx", axis=0, tiled=True),
        preferred_element_type=jnp.float32,
    )
    first = rows.astype(jnp.float32) + attn
    ffn_in = rms_scale(first, gain_ffn).astype(jnp.bfloat16)
    expert_here = w_in.shape[0]
    owners = dp_count * ctx_count
    experts_all = expert_here * owners
    capacity = 2 * keep_here // experts_all
    labels = expert_ids[0, :, 0]
    choose = (labels[:, None] == jnp.arange(experts_all, dtype=jnp.int32)[None, :]).astype(
        jnp.float32
    )
    order = jnp.arange(keep_here, dtype=jnp.int32)
    earlier = (order[None, :] < order[:, None]).astype(jnp.float32)
    before = jnp.dot(earlier, choose, precision=lax.Precision.HIGHEST)
    slots = jnp.sum(before * choose, axis=1).astype(jnp.int32)
    place = labels * capacity + slots
    spots = (place[None, :] == jnp.arange(experts_all * capacity, dtype=jnp.int32)[:, None]).astype(
        jnp.bfloat16
    )
    buffer = jnp.dot(spots, ffn_in, preferred_element_type=jnp.float32).astype(jnp.bfloat16)
    buffer = buffer.reshape(experts_all, capacity, width_model)
    received = lax.all_to_all(buffer, ("dp", "ctx"), split_axis=0, concat_axis=0, tiled=True)
    items = received.shape[1]
    grouped = received.reshape(owners, expert_here, items, width_model)
    hidden = jnp.einsum("sgid,gdf->sgif", grouped, w_in, preferred_element_type=jnp.float32)
    hidden = jnp.maximum(hidden, 0.0).astype(jnp.bfloat16)
    answer = jnp.einsum("sgif,gfd->sgid", hidden, w_back, preferred_element_type=jnp.float32)
    answered = answer.astype(jnp.bfloat16).reshape(owners * expert_here, items, width_model)
    back = lax.all_to_all(answered, ("dp", "ctx"), split_axis=0, concat_axis=0, tiled=True)
    answers = back.reshape(experts_all * capacity, width_model)
    taken = jnp.take(answers, place, axis=0)
    second = (first + taken.astype(jnp.float32)).astype(jnp.bfloat16)
    blended = document.at[local].set(second)
    return blended[None]


def solution(mesh):
    return jax.shard_map(
        body,
        mesh=mesh,
        in_specs=(
            P("dp", "ctx", None),
            P("dp", "ctx"),
            P(),
            P(),
            P(None, "ctx"),
            P(None, "ctx"),
            P(None, "ctx"),
            P("ctx", None),
            P("dp", "ctx", None),
            P(("dp", "ctx"), None, None),
            P(("dp", "ctx"), None, None),
        ),
        out_specs=P("dp", "ctx", None),
        check_vma=False,
    )
```

profile of v0, /device:TPU:0, one launch (start us, length us, event | category | flops | bytes accessed | tf_op | source)
XLA Modules:
  0.0 187.0 jit_solution(8353089613753174881)
XLA Ops:
  6.5 1.2 copy.44
  7.8 1.8 pad_maximum_fusion
  10.3 1.2 gather_fusion
  11.8 32.9 %all-gather.3.cloned.1.call-done = bf16[1024,3,512]{0,2,1:T(8,128)(2,1)} async-done(((bf16[1024,3,64]{0,2,1:T(8,128)(2,1)}), bf16[1024,3,512]{0,2,1:T(8,128)(2,1)}) %all-gather.3.cloned.1.call-update) | async-done | bytes 3145744 | tf_op jit(solution)/shard_map/all_gather | solution.py:57
  44.7 3.0 %convolution_convert_fusion.1 = bf16[256,3,512]{2,0,1:T(8,128)(2,1)S(1)} fusion(bf16[1024,3,512]{0,2,1:T(8,128)(2,1)} %all-gather.3.cloned.1.call-done, f32[1024]{0:T(1024)S(1)} %copy-done.3, f32[256]{0:T(256)S(1)} %add_rsqrt_fusion.1, bf16[256,1024]{1,0:T(8,128)(2,1)S(1)} %gather_fusion, pred[256]{0:T(512)(128)(4,1)S(1)} %compare_and_fusion.1), kind=kOutput, calls=%fused_computation.28 | convolution fusion | flops 807010304 | bytes 4461824 | tf_op jit(solution)/shard_map/td,dcf->tcf/dot_general | solution.py:54
  48.0 0.9 copy.23
  48.9 3.5 %all-to-all-start = ((bf16[256,3,8,64]{0,3,1,2:T(8,128)(2,1)}), bf16[256,3,8,64]{0,3,1,2:T(8,128)(2,1)S(1)}, u32[]{:S(2)}, u32[]{:S(2)}) async-start(bf16[256,3,8,64]{0,3,1,2:T(8,128)(2,1)} %copy.23), calls=%async_computation | async-start | bytes 1572864 | tf_op jit(solution)/shard_map/all_to_all | solution.py:61
  53.2 11.7 %all-to-all-done = bf16[256,3,8,64]{0,3,1,2:T(8,128)(2,1)S(1)} async-done(((bf16[256,3,8,64]{0,3,1,2:T(8,128)(2,1)}), bf16[256,3,8,64]{0,3,1,2:T(8,128)(2,1)S(1)}, u32[]{:S(2)}, u32[]{:S(2)}) %all-to-all-start) | async-done | bytes 786464 | tf_op jit(solution)/shard_map/all_to_all | solution.py:61
  65.3 11.1 %while.10 = (s32[]{:T(128)}, bf16[4,512,1,64]{1,3,2,0:T(8,128)(2,1)S(1)}, bf16[4,512,1,64]{1,3,2,0:T(8,128)(2,1)S(1)}, bf16[2048,1,64]{0,2,1:T(8,128)(2,1)S(1)}, bf16[2048,1,64]{0,2,1:T(8,128)(2,1)S(1)}, /*index=5*/s32[]{:T(128)}) while((s32[]{:T(128)}, bf16[4,512,1,64]{1,3,2,0:T(8,128)(2,1)S(1)}, bf16[4,512,1,64]{1,3,2,0:T(8,128)(2,1)S(1)}, ...), condition=%wide.region_4.6_spmd, body=%wide.region_1.5_spmd.sunk | while | flops 277904384 | bytes 13248589 | solution.py:37
  67.0 1.1 fusion.50
  69.8 1.1 fusion.50
  72.6 1.1 fusion.50
  75.3 1.1 fusion.50
  77.5 11.5 %reduce.4 = bf16[2048,64]{1,0:T(8,128)(2,1)S(1)} reduce(bf16[2048,1,64]{2,1,0:T(2,128)(2,1)S(1)} %reshape.159, bf16[]{:T(256)} %broadcast.107), dimensions={1}, to_apply=%reshape.159.reduce_sub_computation | reduce | bytes 524290 | tf_op jit(solution)/shard_map/reshape | solution.py:37
  89.1 1.1 reshape.170
  90.2 3.6 %all-to-all-start.1 = ((bf16[8,2,8192]{2,1,0:T(2,128)(2,1)}), bf16[8,2,8192]{2,1,0:T(2,128)(2,1)S(1)}, u32[]{:S(2)}, u32[]{:S(2)}) async-start(bf16[8,2,8192]{2,1,0:T(2,128)(2,1)} %reshape.170), calls=%async_computation.1 | async-start | bytes 524288 | tf_op jit(solution)/shard_map/all_to_all | solution.py:63
  94.0 6.4 %all-to-all-done.1 = bf16[8,2,8192]{2,1,0:T(2,128)(2,1)S(1)} async-done(((bf16[8,2,8192]{2,1,0:T(2,128)(2,1)}), bf16[8,2,8192]{2,1,0:T(2,128)(2,1)S(1)}, u32[]{:S(2)}, u32[]{:S(2)}) %all-to-all-start.1) | async-done | bytes 262176 | tf_op jit(solution)/shard_map/all_to_all | solution.py:63
  101.8 1.8 multiply_reduce_fusion.1
  104.2 29.7 %all_to_all.43 = bf16[32,16,1024]{2,1,0:T(8,128)(2,1)S(1)} all-to-all(bf16[32,16,1024]{2,1,0:T(8,128)(2,1)S(1)} %bitcast.94), channel_id=1, replica_groups=mesh['dp'=4,'ctx'=8] {'dp','ctx'}, dimensions={0} | all-to-all | bytes 2097152 | tf_op jit(solution)/shard_map/all_to_all | solution.py:90
  133.9 11.4 %fusion.18 = bf16[32,16,1024]{2,1,0:T(8,128)(2,1)} fusion(bf16[1,2816,1024]{2,1,0:T(8,128)(2,1)} %param.25, bf16[32,16,1024]{2,1,0:T(8,128)(2,1)S(1)} %all_to_all.43, bf16[1,1024,2816]{2,1,0:T(8,128)(2,1)} %param.24), kind=kOutput, calls=%fused_computation.26 | convolution fusion | flops 5908987904 | bytes 13631488 | tf_op jit(solution)/shard_map/sgif,gfd->sgid/dot_general | solution.py:95
  145.3 3.6 %all-to-all-start.3 = ((bf16[32,16,1024]{2,1,0:T(8,128)(2,1)}), bf16[32,16,1024]{2,1,0:T(8,128)(2,1)S(1)}, u32[]{:S(2)}, u32[]{:S(2)}) async-start(bf16[32,16,1024]{2,1,0:T(8,128)(2,1)} %fusion.18), calls=%async_computation.3 | async-start | bytes 2097152 | tf_op jit(solution)/shard_map/all_to_all | solution.py:97
  148.9 26.2 %all-to-all-done.3 = bf16[32,16,1024]{2,1,0:T(8,128)(2,1)S(1)} async-done(((bf16[32,16,1024]{2,1,0:T(8,128)(2,1)}), bf16[32,16,1024]{2,1,0:T(8,128)(2,1)S(1)}, u32[]{:S(2)}, u32[]{:S(2)}) %all-to-all-start.3) | async-done | bytes 1048608 | tf_op jit(solution)/shard_map/all_to_all | solution.py:97
  175.1 4.1 %scatter_custom_fusion = bf16[512,1024]{1,0:T(8,128)(2,1)S(1)} fusion(bf16[512,1024]{1,0:T(8,128)(2,1)S(1)} %bitcast.92, s32[256]{0:T(256)S(1)} %bitcast.106, f32[256,1024]{1,0:T(8,128)S(1)} %get-tuple-element.69, pred[256]{0:T(512)(128)(4,1)S(1)} %compare_and_fusion, bf16[]{:T(256)} %constant.10.clone.2, bf16[512,1024]{1,0:T(8,128)(2,1)S(1)} %bitcast.93, ...), kind=kCustom, calls=%fused_computation.37 | custom fusion | flops 1048576 | bytes 3150338 | tf_op jit(solution)/shard_map/scatter | solution.py:101
  179.2 1.0 copy-done
  (45 shorter events, 12.1 us)
Async XLA Ops:
  6.5 38.1 %copy-start.3 = (f32[1024]{0:T(1024)S(1)}, f32[1024]{0:T(1024)}, u32[]{:S(2)}) copy-start(f32[1024]{0:T(1024)} %param.17) | copy-start | bytes 12292
  6.5 38.1 %all-gather.3.cloned.1.call-start = ((), (), s32[]{:S(2)}) async-start(), calls=%async_computation.4 | async-start | bytes 3538944 | tf_op jit(solution)/shard_map/all_gather | solution.py:57
  48.9 16.1 %all-to-all-start = ((bf16[256,3,8,64]{0,3,1,2:T(8,128)(2,1)}), bf16[256,3,8,64]{0,3,1,2:T(8,128)(2,1)S(1)}, u32[]{:S(2)}, u32[]{:S(2)}) async-start(bf16[256,3,8,64]{0,3,1,2:T(8,128)(2,1)} %copy.23), calls=%async_computation | async-start | bytes 1572864 | tf_op jit(solution)/shard_map/all_to_all | solution.py:61
  52.4 49.4 %all-gather.5.cloned.1.call-start = ((), (), s32[]{:S(2)}) async-start(), calls=%async_computation.5 | async-start | bytes 1179648 | tf_op jit(solution)/shard_map/all_gather | solution.py:67
  76.5 17.3 %copy-start.2 = (s32[1,256,1]{1,2,0:T(1,128)S(1)}, s32[1,256,1]{1,2,0:T(1,128)}, u32[]{:S(2)}) copy-start(s32[1,256,1]{1,2,0:T(1,128)} %param.23) | copy-start | bytes 3076
  89.1 14.5 %copy-start.1 = (f32[1024]{0:T(1024)S(1)}, f32[1024]{0:T(1024)}, u32[]{:S(2)}) copy-start(f32[1024]{0:T(1024)} %param.18) | copy-start | bytes 12292
  90.2 10.3 %all-to-all-start.1 = ((bf16[8,2,8192]{2,1,0:T(2,128)(2,1)}), bf16[8,2,8192]{2,1,0:T(2,128)(2,1)S(1)}, u32[]{:S(2)}, u32[]{:S(2)}) async-start(bf16[8,2,8192]{2,1,0:T(2,128)(2,1)} %reshape.170), calls=%async_computation.1 | async-start | bytes 524288 | tf_op jit(solution)/shard_map/all_to_all | solution.py:63
  145.3 29.8 %all-to-all-start.3 = ((bf16[32,16,1024]{2,1,0:T(8,128)(2,1)}), bf16[32,16,1024]{2,1,0:T(8,128)(2,1)S(1)}, u32[]{:S(2)}, u32[]{:S(2)}) async-start(bf16[32,16,1024]{2,1,0:T(8,128)(2,1)} %fusion.18), calls=%async_computation.3 | async-start | bytes 2097152 | tf_op jit(solution)/shard_map/all_to_all | solution.py:97
  179.2 1.0 copy-start
Sparse Core Ops, SparseCore 0:
  9.7 34.8 all-gather.2
  55.2 24.7 all-gather.4
where the time goes:
time: 188 us; the launch traced here: 187 us
  waiting for transfers between devices  78 us (41%)
  blocking collectives  29.7 us (16%)
  matrix products  24.7 us (13%)
  other arithmetic  21.8 us (12%)
  between operations  13.6 us (7%)
  starting transfers between devices  10.8 us (6%)
  local copies, waits for them, and re-layouts  8.41 us (4%)
    all_gather x1, waiting for transfers between devices, body(): lax.all_gather(stacked, 'ctx', axis=2, tiled=True)  32.9 us
    all_to_all x1, blocking collectives, body(): lax.all_to_all(buffer, ('dp', 'ctx'), split_axis=0, concat_axis=0, tiled=...  29.7 us
    all_to_all x1, waiting for transfers between devices, body(): lax.all_to_all(answered, ('dp', 'ctx'), split_axis=0, concat_axis=0, tile...  26.2 us
    all_to_all x1, waiting for transfers between devices, body(): lax.all_to_all(triple, 'ctx', split_axis=2, concat_axis=0, tiled=True)  11.7 us
    reshape x1, other arithmetic, attend(): return lax.map(one_block, blocks).reshape(count, heads_here, width)  11.5 us
    dot_general x1, matrix products, body(): jnp.einsum('sgif,gfd->sgid', hidden, w_back, preferred_element_type=jnp.f...  11.4 us
    all_to_all x1, waiting for transfers between devices, body(): lax.all_to_all(mixed, 'ctx', split_axis=0, concat_axis=1, tiled=True)  6.43 us
    dot_general x4, matrix products, one_block(): jnp.einsum('hqk,khd->qhd', probs, values, preferred_element_type=jnp.floa...  4.47 us
  transfers between devices with their start and end apart: 5, of which 4 were waited for; matrix products, arithmetic and copies ran while one was open for 15% of the time, Pallas kernels for 0%

commit v1 on v0

v1 whole, which is shorter than its diff:
```python
import functools
import math

import jax
import jax.numpy as jnp
from jax import lax
from jax.experimental import pallas as pl
from jax.experimental.pallas import tpu as pltpu
from jax.sharding import PartitionSpec as P

HS = 64
MESH = pl.DeviceIdType.MESH

eps_norm = 1e-06
score_gain = 2.5


def rms_scale(values, gain):
    values = values.astype(jnp.float32)
    power = jnp.mean(values * values, axis=-1, keepdims=True)
    return values * lax.rsqrt(power + eps_norm) * gain


class Gather:
    def __init__(self, n, me, own, slots, send, recv):
        self.n, self.me, self.own, self.slots = n, me, own, slots
        self.send, self.recv = send, recv
        self.core, self.chip = me % 2, me // 2
        self.partner = me + 1 - 2 * self.core
        self.started = []

    def copy(self, ident, src, dst, target):
        return pltpu.make_async_remote_copy(
            src_ref=src,
            dst_ref=dst,
            send_sem=self.send.at[ident],
            recv_sem=self.recv.at[ident],
            device_id={"ctx": target},
            device_id_type=MESH,
        )

    def peers(self):
        chips = self.n // 2
        if chips == 4:
            x, y = self.chip % 2, self.chip // 2
            nx, ny = y * 2 + (1 - x), (1 - y) * 2 + x
            return [(nx, nx), (ny, ny)]
        return [
            ((self.chip + d) % chips, (self.chip + chips - d) % chips) for d in range(1, chips)
        ]

    def begin(self):
        own_to = self.slots.at[self.me]
        self.first = [
            self.copy(i, self.own, own_to, to * 2 + self.core)
            for i, (to, _) in enumerate(self.peers())
        ]
        self.base = len(self.first)
        self.twin = self.copy(self.base, self.own, own_to, self.partner)
        for c in self.first:
            c.start()
        self.twin.start()
        self.started = self.first + [self.twin]

    def relay(self):
        here, self.passed, self.late = [], [], []
        ident = self.base + 1
        peers = self.peers()
        square = self.n // 2 == 4
        half = self.own.shape[0] // 2
        for i, (_, source) in enumerate(peers):
            self.first[i].wait_recv()
            block = source * 2 + self.core
            here.append(block)
            if square:
                piece = self.slots.at[block, pl.ds(i * half, half)]
                c = self.copy(ident, piece, piece, peers[1 - i][0] * 2 + self.core)
                c.start()
                self.late.append(c)
                ident += 1
            c = self.copy(ident, self.slots.at[block], self.slots.at[block], self.partner)
            c.start()
            self.passed.append((source * 2 + 1 - self.core, c))
            ident += 1
        self.ident = ident
        self.started += self.late + [c for _, c in self.passed]
        return here

    def diagonal(self):
        if not self.late:
            return None
        block = (3 - self.chip) * 2 + self.core
        half = self.own.shape[0] // 2
        self.last = []
        for i, c in enumerate(self.late):
            c.wait_recv()
            piece = self.slots.at[block, pl.ds(i * half, half)]
            c = self.copy(self.ident + i, piece, piece, self.partner)
            c.start()
            self.last.append(c)
        self.started += self.last
        return block

    def final(self):
        if not self.late:
            return None
        for c in self.last:
            c.wait_recv()
        return (3 - self.chip) * 2 + 1 - self.core

    def drain(self):
        for c in self.started:
            c.wait_send()


def gather_copies(n):
    return 9 if n // 2 == 4 else 2 * (n // 2) - 1


def attention_kernel(
    n,
    heads,
    x_ref,
    wq_ref,
    wk_ref,
    wv_ref,
    wo_ref,
    mixed_ref,
    wo_all,
    x_all,
    q_all,
    k_all,
    v_all,
    stage,
    x_send,
    x_recv,
    o_send,
    o_recv,
    m_send,
    m_recv,
):
    me = lax.axis_index("ctx")
    rows = x_ref.shape[0]
    barrier = pltpu.get_barrier_semaphore()
    for d in range(1, n):
        pl.semaphore_signal(
            barrier, inc=1, device_id={"ctx": (me + d) % n}, device_id_type=MESH
        )
    pl.semaphore_wait(barrier, n - 1)

    def project(block, value):
        at = pl.ds(pl.multiple_of(block * rows, rows), rows)
        for h in range(heads):
            cols = pl.ds(h * HS, HS)
            q_all[h, at, :] = jnp.dot(
                value, wq_ref[:, cols], preferred_element_type=jnp.float32
            ).astype(jnp.bfloat16)
            k_all[h, at, :] = jnp.dot(
                value, wk_ref[:, cols], preferred_element_type=jnp.float32
            ).astype(jnp.bfloat16)
        v_all[:, at] = lax.dot_general(
            wv_ref[...], value, (((1,), (1,)), ((), ())), preferred_element_type=jnp.float32
        ).astype(jnp.bfloat16)

    g = Gather(n, me, x_ref, x_all, x_send, x_recv)
    o = Gather(n, me, wo_ref, wo_all, o_send, o_recv)
    g.begin()
    project(me, x_ref[...])
    wo_all[me] = wo_ref[...]
    g.twin.wait_recv()
    project(g.partner, x_all[g.partner])
    here = g.relay()
    o.begin()
    for block in here:
        project(block, x_all[block])
    for block, c in g.passed:
        c.wait_recv()
        project(block, x_all[block])
    block = g.diagonal()
    if block is not None:
        project(block, x_all[block])
    o.twin.wait_recv()
    o.relay()
    block = g.final()
    if block is not None:
        project(block, x_all[block])

    scale = score_gain / math.sqrt(HS) * math.log2(math.e)

    def send_block(step, target):
        return pltpu.make_async_remote_copy(
            src_ref=stage.at[step],
            dst_ref=mixed_ref.at[me],
            send_sem=m_send.at[step],
            recv_sem=m_recv.at[step],
            device_id={"ctx": target},
            device_id_type=MESH,
        )

    @pl.loop(0, n)
    def _(step):
        block = lax.rem(me + 1 + step, n)
        at = pl.ds(pl.multiple_of(block * rows, rows), rows)
        for h in range(heads):
            scores = lax.dot_general(
                k_all[h],
                q_all[h, at, :],
                (((1,), (1,)), ((), ())),
                preferred_element_type=jnp.float32,
            )
            top = jnp.max(scores, axis=0, keepdims=True)
            weights = jnp.exp2(scores * scale - top * scale)
            total = jnp.sum(weights, axis=0, keepdims=True)
            cols = pl.ds(h * HS, HS)
            mixed = jnp.dot(
                v_all[cols, :],
                weights.astype(jnp.bfloat16),
                preferred_element_type=jnp.float32,
            )
            stage[step, cols, :] = (mixed / total).astype(jnp.bfloat16)

        @pl.when(step < n - 1)
        def _():
            send_block(step, block).start()

    mixed_ref[me] = stage[n - 1]
    for _, c in o.passed:
        c.wait_recv()
    o.diagonal()
    o.final()

    @pl.loop(0, n - 1)
    def _(step):
        send_block(step, lax.rem(me + 1 + step, n)).wait()

    g.drain()
    o.drain()


def attention(normed, w_query, w_key, w_value, w_out):
    n = lax.axis_size("ctx")
    rows, width = normed.shape
    inner = w_query.shape[1]
    heads = inner // HS
    copies = gather_copies(n)
    vmem = pl.BlockSpec(memory_space=pltpu.VMEM)
    bf = jnp.bfloat16
    return pl.pallas_call(
        functools.partial(attention_kernel, n, heads),
        out_shape=(
            jax.ShapeDtypeStruct((n, inner, rows), bf),
            jax.ShapeDtypeStruct((n,) + w_out.shape, bf),
        ),
        in_specs=[vmem] * 5,
        out_specs=(vmem, vmem),
        scratch_shapes=[
            pltpu.VMEM((n, rows, width), bf),
            pltpu.VMEM((heads, n * rows, HS), bf),
            pltpu.VMEM((heads, n * rows, HS), bf),
            pltpu.VMEM((inner, n * rows), bf),
            pltpu.VMEM((n, inner, rows), bf),
            pltpu.SemaphoreType.DMA((copies,)),
            pltpu.SemaphoreType.DMA((copies,)),
            pltpu.SemaphoreType.DMA((copies,)),
            pltpu.SemaphoreType.DMA((copies,)),
            pltpu.SemaphoreType.DMA((n,)),
            pltpu.SemaphoreType.DMA((n,)),
        ],
        compiler_params=pltpu.CompilerParams(collective_id=0, has_side_effects=True),
        name="attention",
    )(normed, w_query, w_key, w_value.T, w_out)


def experts(buffer, w_in, w_back, capacity):
    owners = lax.axis_size("dp") * lax.axis_size("ctx")
    expert_here, width = w_in.shape[0], buffer.shape[1]
    buffer = buffer.reshape(owners * expert_here, capacity, width)
    received = lax.all_to_all(buffer, ("dp", "ctx"), split_axis=0, concat_axis=0, tiled=True)
    grouped = received.reshape(owners, expert_here, capacity, width)
    hidden = jnp.einsum("sgid,gdf->sgif", grouped, w_in, preferred_element_type=jnp.float32)
    hidden = jnp.maximum(hidden, 0.0).astype(jnp.bfloat16)
    answer = jnp.einsum("sgif,gfd->sgid", hidden, w_back, preferred_element_type=jnp.float32)
    answered = answer.astype(jnp.bfloat16).reshape(owners * expert_here, capacity, width)
    back = lax.all_to_all(answered, ("dp", "ctx"), split_axis=0, concat_axis=0, tiled=True)
    return back.reshape(owners * expert_here * capacity, width)


def body(
    tokens, kept, gain_attn, gain_ffn, w_query, w_key, w_value, w_out, expert_ids, w_in, w_back
):
    document = tokens[0]
    shard_len, width_model = document.shape
    ctx_count = lax.axis_size("ctx")
    dp_count = lax.axis_size("dp")
    local = kept[0] - lax.axis_index("ctx") * shard_len
    keep_here = local.shape[0]
    rows = jnp.take(document, local, axis=0)
    normed = rms_scale(rows, gain_attn).astype(jnp.bfloat16)
    mixed, w_out_all = attention(normed, w_query, w_key, w_value, w_out)
    inner_all = w_out.shape[0] * ctx_count
    attn = lax.dot_general(
        mixed.reshape(inner_all, keep_here),
        w_out_all.reshape(inner_all, width_model),
        (((0,), (0,)), ((), ())),
        preferred_element_type=jnp.float32,
    )
    first = rows.astype(jnp.float32) + attn
    ffn_in = rms_scale(first, gain_ffn).astype(jnp.bfloat16)
    expert_here = w_in.shape[0]
    owners = dp_count * ctx_count
    experts_all = expert_here * owners
    capacity = 2 * keep_here // experts_all
    labels = expert_ids[0, :, 0]
    order = jnp.arange(keep_here, dtype=jnp.int32)
    same = (labels[:, None] == labels[None, :]) & (order[None, :] < order[:, None])
    slots = jnp.sum(same.astype(jnp.int32), axis=1)
    place = labels * capacity + slots
    cells = jnp.arange(experts_all * capacity, dtype=jnp.int32)
    spots = (place[None, :] == cells[:, None]).astype(jnp.bfloat16)
    buffer = jnp.dot(spots, ffn_in, preferred_element_type=jnp.float32).astype(jnp.bfloat16)
    answers = experts(buffer, w_in, w_back, capacity)
    seats = (place[:, None] == cells[None, :]).astype(jnp.bfloat16)
    taken = jnp.dot(seats, answers, preferred_element_type=jnp.float32)
    second = (first + taken).astype(jnp.bfloat16)
    hits = jnp.arange(shard_len, dtype=jnp.int32)[:, None] == local[None, :]
    fresh = jnp.dot(hits.astype(jnp.bfloat16), second, preferred_element_type=jnp.float32)
    touched = jnp.any(hits, axis=1, keepdims=True)
    blended = jnp.where(touched, fresh.astype(jnp.bfloat16), document)
    return blended[None]


def solution(mesh):
    return jax.shard_map(
        body,
        mesh=mesh,
        in_specs=(
            P("dp", "ctx", None),
            P("dp", "ctx"),
            P(),
            P(),
            P(None, "ctx"),
            P(None, "ctx"),
            P(None, "ctx"),
            P("ctx", None),
            P("dp", "ctx", None),
            P(("dp", "ctx"), None, None),
            P(("dp", "ctx"), None, None),
        ),
        out_specs=P("dp", "ctx", None),
        check_vma=False,
    )
```

time: 188 us -> 128 us (0.68)
  waiting for transfers between devices: 78 us -> 26 us
  Pallas kernels: 0 us -> 41.5 us
  other arithmetic: 21.8 us -> 2.41 us
  between operations: 13.6 us -> 0.09 us
  matrix products: 24.7 us -> 15.6 us
  starting transfers between devices: 10.8 us -> 3.63 us
  local copies, waits for them, and re-layouts: 8.41 us -> 6.47 us
    pallas_call x0 -> x1, Pallas kernels: none -> 41.5 us  [attention(): pl.pallas_call(functools.partial(attention_kernel, n, heads), out_shape=(...]
    all_gather x2 -> x0, waiting for transfers between devices: 32.9 us -> none  [the longest x1 32.9 us: body(): lax.all_gather(stacked, 'ctx', axis=2, tiled=True)]
    all_to_all x3 -> x1, waiting for transfers between devices: 44.3 us -> 26 us  [experts(): lax.all_to_all(answered, ('dp', 'ctx'), split_axis=0, concat_axis=0, tile...]
    reshape x1 -> x0, other arithmetic: 11.5 us -> none  [attend(): return lax.map(one_block, blocks).reshape(count, heads_here, width)]
    dot_general x12 -> x3, matrix products: 24.1 us -> 15.1 us  [the longest x1 11.5 us: experts(): jnp.einsum('sgif,gfd->sgid', hidden, w_back, preferred_element_type=jnp.f...]
    all_to_all x3 -> x1, starting transfers between devices: 10.8 us -> 3.63 us  [experts(): lax.all_to_all(answered, ('dp', 'ctx'), split_axis=0, concat_axis=0, tile...]
    scatter x1 -> x0, other arithmetic: 4.11 us -> none  [body(): blended = document.at[local].set(second)]
    reduce_sum x4 -> x1, other arithmetic: 3.3 us -> 0.18 us  [body(): slots = jnp.sum(same.astype(jnp.int32), axis=1)]
  transfers between devices with their start and end apart: 5 -> 1, of which waited for: 4 -> 1; matrix products, arithmetic and copies ran while one was open for 15% -> 0% of each run, Pallas kernels for 0% -> 0%
where the time goes in v1:
time: 128 us; the launch traced here: 127 us
  Pallas kernels  41.5 us (32%)
  blocking collectives  31.5 us (25%)
  waiting for transfers between devices  26 us (20%)
  matrix products  15.6 us (12%)
  local copies, waits for them, and re-layouts  6.47 us (5%)
  starting transfers between devices  3.63 us (3%)
  other arithmetic  2.41 us (2%)
    pallas_call x1, Pallas kernels, attention(): pl.pallas_call(functools.partial(attention_kernel, n, heads), out_shape=(...  41.5 us
    all_to_all x1, blocking collectives, experts(): lax.all_to_all(buffer, ('dp', 'ctx'), split_axis=0, concat_axis=0, tiled=...  31.5 us
    all_to_all x1, waiting for transfers between devices, experts(): lax.all_to_all(answered, ('dp', 'ctx'), split_axis=0, concat_axis=0, tile...  26 us
    dot_general x1, matrix products, experts(): jnp.einsum('sgif,gfd->sgid', hidden, w_back, preferred_element_type=jnp.f...  11.5 us
    all_to_all x1, starting transfers between devices, experts(): lax.all_to_all(answered, ('dp', 'ctx'), split_axis=0, concat_axis=0, tile...  3.63 us
    unnamed x10, local copies, waits for them, and re-layouts  3.55 us
    gather x1, local copies, waits for them, and re-layouts, body(): rows = jnp.take(document, local, axis=0)  2.93 us
  transfers between devices with their start and end apart: 1, of which 1 were waited for; matrix products, arithmetic and copies ran while one was open for 0% of the time, Pallas kernels for 0%

profile of v1, /device:TPU:0, one launch (start us, length us, event | category | flops | bytes accessed | tf_op | source)
XLA Modules:
  0.0 127.2 jit_solution(3344393650520180391)
XLA Ops:
  0.0 0.0 copy-start.2
  0.0 0.7 compare_select_fusion
  0.7 0.0 copy-start.1
  0.7 0.0 copy-start.3
  0.7 2.9 %gather_fusion = bf16[256,1024]{1,0:T(8,128)(2,1)S(1)} fusion(bf16[512,1024]{1,0:T(8,128)(2,1)} %bitcast.34, s32[1024]{0:T(1024)S(1)} %pad_clamp_fusion), kind=kCustom, calls=%fused_computation | custom fusion | bytes 1049600 | tf_op jit(solution)/shard_map/jit(_take)/gather | solution.py:297
  3.7 0.3 fusion.12
  4.0 1.8 %copy.16.wq_ref = bf16[1024,64]{1,0:T(8,128)(2,1)} copy(bf16[1024,64]{0,1:T(8,128)(2,1)} %param.15) | data formatting | bytes 262144 | tf_op args[4]
  5.7 1.8 %copy.17.wk_ref = bf16[1024,64]{1,0:T(8,128)(2,1)} copy(bf16[1024,64]{0,1:T(8,128)(2,1)} %param.16) | data formatting | bytes 262144 | tf_op args[5]
  7.5 0.0 copy-done.2
  7.5 1.1 fusion.14.x_ref
  8.6 41.5 %attention.1 = (bf16[8,64,256]{2,1,0:T(8,128)(2,1)}, bf16[8,64,1024]{2,1,0:T(8,128)(2,1)}) custom-call(bf16[256,1024]{1,0:T(8,128)(2,1)} %fusion.14.x_ref, bf16[1024,64]{1,0:T(8,128)(2,1)} %copy.16.wq_ref, bf16[1024,64]{1,0:T(8,128)(2,1)} %copy.17.wk_ref, bf16[64,1024]{1,0:T(8,128)(2,1)} %bitcast.37, bf16[64,1024]{1,0:T(8,128)(2,1)} %wo_ref.1), custom_call_target="tpu_custom_call" | custom-call | tf_op jit(solution)/shard_map/attention/pallas_call | solution.py:248
  50.0 1.9 %multiply_reduce_fusion = (f32[256]{0:T(256)S(1)}, f32[256,1024]{1,0:T(8,128)S(1)}) fusion(bf16[8,64,256]{2,1,0:T(8,128)(2,1)} %get-tuple-element.7, bf16[8,64,1024]{2,1,0:T(8,128)(2,1)} %get-tuple-element.8, bf16[256,1024]{1,0:T(8,128)(2,1)S(1)} %gather_fusion, pred[256]{0:T(512)(128)(4,1)S(1)} %compare_and_fusion), kind=kOutput, calls=%fused_computation.21 | convolution fusion | flops 269745920 | bytes 2884864 | tf_op jit(solution)/shard_map/dot_general | solution.py:301
  51.9 0.0 copy-done.1
  51.9 0.2 convert_reduce_fusion
  52.1 0.0 copy-done.3
  52.1 0.5 convolution_convert_fusion.1
  52.7 31.5 %all_to_all.10 = bf16[32,16,1024]{2,1,0:T(8,128)(2,1)S(1)} all-to-all(bf16[32,16,1024]{2,1,0:T(8,128)(2,1)S(1)} %bitcast.35), channel_id=1, replica_groups=mesh['dp'=4,'ctx'=8] {'dp','ctx'}, dimensions={0} | all-to-all | bytes 2097152 | tf_op jit(solution)/shard_map/all_to_all | solution.py:278
  84.1 0.0 copy-start
  84.1 11.5 %fusion.6 = bf16[32,16,1024]{2,1,0:T(8,128)(2,1)} fusion(bf16[1,2816,1024]{2,1,0:T(8,128)(2,1)} %param.21, bf16[32,16,1024]{2,1,0:T(8,128)(2,1)S(1)} %all_to_all.10, bf16[1,1024,2816]{2,1,0:T(8,128)(2,1)} %param.20), kind=kOutput, calls=%fused_computation.9 | convolution fusion | flops 5908987904 | bytes 13631488 | tf_op jit(solution)/shard_map/sgif,gfd->sgid/dot_general | solution.py:282
  95.6 3.6 %all-to-all-start.1 = ((bf16[32,16,1024]{2,1,0:T(8,128)(2,1)}), bf16[32,16,1024]{2,1,0:T(8,128)(2,1)S(1)}, u32[]{:S(2)}, u32[]{:S(2)}) async-start(bf16[32,16,1024]{2,1,0:T(8,128)(2,1)} %fusion.6), calls=%async_computation.1 | async-start | bytes 2097152 | tf_op jit(solution)/shard_map/all_to_all | solution.py:284
  99.2 0.2 fusion.19
  99.4 26.0 %all-to-all-done.1 = bf16[32,16,1024]{2,1,0:T(8,128)(2,1)S(1)} async-done(((bf16[32,16,1024]{2,1,0:T(8,128)(2,1)}), bf16[32,16,1024]{2,1,0:T(8,128)(2,1)S(1)}, u32[]{:S(2)}, u32[]{:S(2)}) %all-to-all-start.1) | async-done | bytes 1048608 | tf_op jit(solution)/shard_map/all_to_all | solution.py:284
  125.4 0.0 copy-done
  125.4 1.7 %fusion.10 = bf16[1,512,1024]{2,1,0:T(8,128)(2,1)} fusion(f32[256,1024]{1,0:T(8,128)S(1)} %get-tuple-element.12, bf16[512,1024]{1,0:T(8,128)(2,1)S(1)} %bitcast.36, pred[512]{0:T(512)(128)(4,1)S(1)} %fusion.19, s32[256]{0:T(256)S(1)} %multiply_add_fusion, s32[256]{0:T(256)S(1)} %bitcast.43, bf16[1,512,1024]{2,1,0:T(8,128)(2,1)S(1)} %copy-done), kind=kOutput, calls=%fused_computation.13 | convolution fusion | flops 538705920 | bytes 4196864 | tf_op jit(solution)/shard_map/dot_general | solution.py:326
  (5 shorter events, 0.0 us)
Async XLA Ops:
  0.0 7.5 %copy-start.2 = (f32[1024]{0:T(1024)S(1)}, f32[1024]{0:T(1024)}, u32[]{:S(2)}) copy-start(f32[1024]{0:T(1024)} %param.13) | copy-start | bytes 12292
  0.7 51.2 %copy-start.1 = (s32[1,256,1]{1,2,0:T(1,128)S(1)}, s32[1,256,1]{1,2,0:T(1,128)}, u32[]{:S(2)}) copy-start(s32[1,256,1]{1,2,0:T(1,128)} %param.19) | copy-start | bytes 3076
  0.7 51.4 %copy-start.3 = (f32[1024]{0:T(1024)S(1)}, f32[1024]{0:T(1024)}, u32[]{:S(2)}) copy-start(f32[1024]{0:T(1024)} %param.14) | copy-start | bytes 12292
  84.1 41.3 %copy-start = (bf16[1,512,1024]{2,1,0:T(8,128)(2,1)S(1)}, bf16[1,512,1024]{2,1,0:T(8,128)(2,1)}, u32[]{:S(2)}) copy-start(bf16[1,512,1024]{2,1,0:T(8,128)(2,1)} %param.11) | copy-start | bytes 3145732
  95.6 29.8 %all-to-all-start.1 = ((bf16[32,16,1024]{2,1,0:T(8,128)(2,1)}), bf16[32,16,1024]{2,1,0:T(8,128)(2,1)S(1)}, u32[]{:S(2)}, u32[]{:S(2)}) async-start(bf16[32,16,1024]{2,1,0:T(8,128)(2,1)} %fusion.6), calls=%async_computation.1 | async-start | bytes 2097152 | tf_op jit(solution)/shard_map/all_to_all | solution.py:284

commit v2 on v1

--- a/solution.py
+++ b/solution.py
@@ -10,6 +10,7 @@
 
 HS = 64
 MESH = pl.DeviceIdType.MESH
+LAST = (((1,), (1,)), ((), ()))
 
 eps_norm = 1e-06
 score_gain = 2.5
@@ -152,14 +153,14 @@
         at = pl.ds(pl.multiple_of(block * rows, rows), rows)
         for h in range(heads):
             cols = pl.ds(h * HS, HS)
-            q_all[h, at, :] = jnp.dot(
-                value, wq_ref[:, cols], preferred_element_type=jnp.float32
+            q_all[h, at, :] = lax.dot_general(
+                value, wq_ref[cols, :], LAST, preferred_element_type=jnp.float32
             ).astype(jnp.bfloat16)
-            k_all[h, at, :] = jnp.dot(
-                value, wk_ref[:, cols], preferred_element_type=jnp.float32
+            k_all[h, at, :] = lax.dot_general(
+                value, wk_ref[cols, :], LAST, preferred_element_type=jnp.float32
             ).astype(jnp.bfloat16)
         v_all[:, at] = lax.dot_general(
-            wv_ref[...], value, (((1,), (1,)), ((), ())), preferred_element_type=jnp.float32
+            wv_ref[...], value, LAST, preferred_element_type=jnp.float32
         ).astype(jnp.bfloat16)
 
     g = Gather(n, me, x_ref, x_all, x_send, x_recv)
@@ -205,7 +206,7 @@
             scores = lax.dot_general(
                 k_all[h],
                 q_all[h, at, :],
-                (((1,), (1,)), ((), ())),
+                LAST,
                 preferred_element_type=jnp.float32,
             )
             top = jnp.max(scores, axis=0, keepdims=True)
@@ -268,10 +269,10 @@
         ],
         compiler_params=pltpu.CompilerParams(collective_id=0, has_side_effects=True),
         name="attention",
-    )(normed, w_query, w_key, w_value.T, w_out)
-
-
-def experts(buffer, w_in, w_back, capacity):
+    )(normed, w_query.T, w_key.T, w_value.T, w_out)
+
+
+def experts_plain(buffer, w_in, w_back, capacity):
     owners = lax.axis_size("dp") * lax.axis_size("ctx")
     expert_here, width = w_in.shape[0], buffer.shape[1]
     buffer = buffer.reshape(owners * expert_here, capacity, width)
@@ -285,6 +286,186 @@
     return back.reshape(owners * expert_here * capacity, width)
 
 
+def expert_kernel(
+    planes,
+    n,
+    cap,
+    buf_ref,
+    w_in_hbm,
+    w_back_hbm,
+    back_ref,
+    w_in_ref,
+    w_back_ref,
+    rows_ref,
+    hidden_ref,
+    answer_ref,
+    w_sem,
+    own_sem,
+    d_send,
+    d_recv,
+    r_send,
+    r_recv,
+):
+    dp, ctx = lax.axis_index("dp"), lax.axis_index("ctx")
+    me = dp * n + ctx
+    owners = planes * n
+    loads = [
+        pltpu.make_async_copy(w_in_hbm.at[0], w_in_ref, w_sem.at[0]),
+        pltpu.make_async_copy(w_back_hbm.at[0], w_back_ref, w_sem.at[1]),
+    ]
+    for c in loads:
+        c.start()
+    barrier = pltpu.get_barrier_semaphore()
+
+    @pl.loop(1, owners)
+    def _(d):
+        to = lax.rem(me + d, owners)
+        pl.semaphore_signal(
+            barrier, inc=1, device_id={"dp": to // n, "ctx": lax.rem(to, n)}, device_id_type=MESH
+        )
+
+    pl.semaphore_wait(barrier, owners - 1)
+
+    def seat(index):
+        return pl.ds(pl.multiple_of(index * cap, cap), cap)
+
+    def at(shift):
+        plane_shift, place_shift = shift // n, lax.rem(shift, n)
+        half = planes // 2
+        side = dp // half
+        side = lax.rem(side + plane_shift // half, 2)
+        plane = side * half + lax.rem(dp + plane_shift, half)
+        return plane, lax.rem(ctx + place_shift, n)
+
+    def dispatch(shift):
+        plane, place = at(shift)
+        return pltpu.make_async_remote_copy(
+            src_ref=buf_ref.at[seat(plane * n + place)],
+            dst_ref=rows_ref.at[seat(me)],
+            send_sem=d_send.at[shift],
+            recv_sem=d_recv.at[shift],
+            device_id={"dp": plane, "ctx": place},
+            device_id_type=MESH,
+        )
+
+    def give_back(shift):
+        plane, place = at(shift)
+        return pltpu.make_async_remote_copy(
+            src_ref=answer_ref.at[seat(plane * n + place)],
+            dst_ref=back_ref.at[seat(me)],
+            send_sem=r_send.at[shift],
+            recv_sem=r_recv.at[shift],
+            device_id={"dp": plane, "ctx": place},
+            device_id_type=MESH,
+        )
+
+    near = owners // 2
+
+    @pl.loop(0, near)
+    def _(shift):
+        dispatch(near + shift).start()
+
+        @pl.when(shift > 0)
+        def _():
+            dispatch(shift).start()
+
+    own_in = pltpu.make_async_copy(buf_ref.at[seat(me)], rows_ref.at[seat(me)], own_sem.at[0])
+    own_in.start()
+
+    def run(first_row, count):
+        inner = hidden_ref.shape[1]
+        width = answer_ref.shape[1]
+        take = pl.ds(pl.multiple_of(first_row, count), count)
+        value = rows_ref[take, :]
+
+        @pl.loop(0, inner // 256)
+        def _(f):
+            cols = pl.ds(pl.multiple_of(f * 256, 256), 256)
+            hidden = jnp.dot(value, w_in_ref[:, cols], preferred_element_type=jnp.float32)
+            hidden_ref[:, cols] = jnp.maximum(hidden, 0.0).astype(jnp.bfloat16)
+
+        @pl.loop(0, width // 256)
+        def _(f):
+            cols = pl.ds(pl.multiple_of(f * 256, 256), 256)
+            answer_ref[take, cols] = jnp.dot(
+                hidden_ref[...], w_back_ref[:, cols], preferred_element_type=jnp.float32
+            ).astype(jnp.bfloat16)
+
+    half_rows = near * cap
+    side = dp // (planes // 2)
+
+    @pl.loop(1, near)
+    def _(shift):
+        dispatch(shift).wait_recv()
+
+    own_in.wait()
+    for c in loads:
+        c.wait()
+
+    @pl.loop(0, 2)
+    def _(turn):
+        @pl.when(turn == 1)
+        def _():
+            @pl.loop(near, owners)
+            def _(shift):
+                dispatch(shift).wait_recv()
+
+        run(lax.rem(side + turn, 2) * half_rows, half_rows)
+
+        @pl.loop(0, near)
+        def _(shift):
+            @pl.when(turn * near + shift > 0)
+            def _():
+                give_back(turn * near + shift).start()
+
+    own_out = pltpu.make_async_copy(answer_ref.at[seat(me)], back_ref.at[seat(me)], own_sem.at[1])
+    own_out.start()
+
+    @pl.loop(1, owners)
+    def _(shift):
+        dispatch(shift).wait_send()
+        give_back(shift).wait()
+
+    own_out.wait()
+
+
+def experts_fused(buffer, w_in, w_back, capacity):
+    planes, n = lax.axis_size("dp"), lax.axis_size("ctx")
+    owners = planes * n
+    slots, width = buffer.shape
+    inner = w_in.shape[2]
+    bf = jnp.bfloat16
+    vmem = pl.BlockSpec(memory_space=pltpu.VMEM)
+    hbm = pl.BlockSpec(memory_space=pl.ANY)
+    return pl.pallas_call(
+        functools.partial(expert_kernel, planes, n, capacity),
+        out_shape=jax.ShapeDtypeStruct((slots, width), bf),
+        in_specs=[vmem, hbm, hbm],
+        out_specs=vmem,
+        scratch_shapes=[
+            pltpu.VMEM(w_in.shape[1:], bf),
+            pltpu.VMEM(w_back.shape[1:], bf),
+            pltpu.VMEM((slots, width), bf),
+            pltpu.VMEM((slots // 2, inner), bf),
+            pltpu.VMEM((slots, width), bf),
+            pltpu.SemaphoreType.DMA((2,)),
+            pltpu.SemaphoreType.DMA((2,)),
+            pltpu.SemaphoreType.DMA((owners,)),
+            pltpu.SemaphoreType.DMA((owners,)),
+            pltpu.SemaphoreType.DMA((owners,)),
+            pltpu.SemaphoreType.DMA((owners,)),
+        ],
+        compiler_params=pltpu.CompilerParams(collective_id=1, has_side_effects=True),
+        name="experts",
+    )(buffer, w_in, w_back)
+
+
+def experts(buffer, w_in, w_back, capacity):
+    if capacity % 16 == 0 and w_in.shape[0] == 1:
+        return experts_fused(buffer, w_in, w_back, capacity)
+    return experts_plain(buffer, w_in, w_back, capacity)
+
+
 def body(
     tokens, kept, gain_attn, gain_ffn, w_query, w_key, w_value, w_out, expert_ids, w_in, w_back
 ):
@@ -294,7 +475,9 @@
     dp_count = lax.axis_size("dp")
     local = kept[0] - lax.axis_index("ctx") * shard_len
     keep_here = local.shape[0]
-    rows = jnp.take(document, local, axis=0)
+    positions = jnp.arange(shard_len, dtype=jnp.int32)
+    picks = (local[:, None] == positions[None, :]).astype(jnp.bfloat16)
+    rows = jnp.dot(picks, document, preferred_element_type=jnp.float32).astype(jnp.bfloat16)
     normed = rms_scale(rows, gain_attn).astype(jnp.bfloat16)
     mixed, w_out_all = attention(normed, w_query, w_key, w_value, w_out)
     inner_all = w_out.shape[0] * ctx_count
@@ -322,7 +505,7 @@
     seats = (place[:, None] == cells[None, :]).astype(jnp.bfloat16)
     taken = jnp.dot(seats, answers, preferred_element_type=jnp.float32)
     second = (first + taken).astype(jnp.bfloat16)
-    hits = jnp.arange(shard_len, dtype=jnp.int32)[:, None] == local[None, :]
+    hits = positions[:, None] == local[None, :]
     fresh = jnp.dot(hits.astype(jnp.bfloat16), second, preferred_element_type=jnp.float32)
     touched = jnp.any(hits, axis=1, keepdims=True)
     blended = jnp.where(touched, fresh.astype(jnp.bfloat16), document)

time: 128 us -> 112 us (0.88)
  the two profiles are of different devices: /device:TPU:0 before, /device:TPU:19 now
where the time goes in v2:
time: 112 us
  Pallas kernels  99.3 us (89%)
  matrix products  8.11 us (7%)
  other arithmetic  4.17 us (4%)
    pallas_call x1, Pallas kernels, experts_fused(): pl.pallas_call(functools.partial(expert_kernel, planes, n, capacity), out...  59.3 us
    pallas_call x1, Pallas kernels, attention(): pl.pallas_call(functools.partial(attention_kernel, n, heads), out_shape=(...  40.1 us
    dot_general x1, matrix products, body(): jnp.dot(hits.astype(jnp.bfloat16), second, preferred_element_type=jnp.flo...  2.96 us

profile of v2, /device:TPU:19, one launch (start us, length us, event | category | flops | bytes accessed | tf_op | source)
XLA Modules:
  0.0 111.7 jit_solution(9422567433725649374)
XLA Ops:
  0.0 0.0 copy-start.1
  0.0 0.7 broadcast_subtract_fusion
  0.7 0.2 fusion.9
  0.9 0.9 convert_reduce_fusion
  1.8 0.7 multiply_add_fusion
  2.5 1.8 %fusion.3 = (f32[256]{0:T(256)S(1)}, bf16[256,1024]{1,0:T(8,128)(2,1)S(1)}) fusion(bf16[1,512,1024]{2,1,0:T(8,128)(2,1)} %param.11, s32[256]{0:T(256)S(1)} %bitcast.26), kind=kOutput, calls=%fused_computation.11 | convolution fusion | flops 269614848 | bytes 1574912 | tf_op jit(solution)/shard_map/dot_general | solution.py:480
  4.3 1.7 %fusion.5.x_ref = bf16[256,1024]{1,0:T(8,128)(2,1)} fusion(bf16[256,1024]{1,0:T(8,128)(2,1)S(1)} %get-tuple-element.10, f32[1024]{0:T(1024)} %param.13, f32[256]{0:T(256)S(1)} %add_rsqrt_fusion.1), kind=kLoop, calls=%fused_computation.13 | loop fusion | flops 1048576 | bytes 1053696 | tf_op jit(solution)/shard_map/convert_element_type | solution.py:481
  6.0 40.1 %attention.1 = (bf16[8,64,256]{2,1,0:T(8,128)(2,1)}, bf16[8,64,1024]{2,1,0:T(8,128)(2,1)}) custom-call(bf16[256,1024]{1,0:T(8,128)(2,1)} %fusion.5.x_ref, bf16[64,1024]{1,0:T(8,128)(2,1)} %bitcast.20, bf16[64,1024]{1,0:T(8,128)(2,1)} %bitcast.21, bf16[64,1024]{1,0:T(8,128)(2,1)} %bitcast.22, bf16[64,1024]{1,0:T(8,128)(2,1)} %wo_ref.1), custom_call_target="tpu_custom_call" | custom-call | tf_op jit(solution)/shard_map/attention/pallas_call | solution.py:249
  46.0 1.9 %multiply_reduce_fusion = (f32[256]{0:T(256)S(1)}, f32[256,1024]{1,0:T(8,128)S(1)}) fusion(bf16[8,64,256]{2,1,0:T(8,128)(2,1)} %get-tuple-element.7, bf16[8,64,1024]{2,1,0:T(8,128)(2,1)} %get-tuple-element.8, bf16[256,1024]{1,0:T(8,128)(2,1)S(1)} %get-tuple-element.10), kind=kOutput, calls=%fused_computation.16 | convolution fusion | flops 269483776 | bytes 2884608 | tf_op jit(solution)/shard_map/dot_general | solution.py:484
  47.9 0.0 copy-done.1
  47.9 1.5 %convolution_convert_fusion.1.buf_ref = bf16[512,1024]{1,0:T(8,128)(2,1)} fusion(f32[256,1024]{1,0:T(8,128)S(1)} %get-tuple-element.12, f32[1024]{0:T(1024)S(1)} %copy-done.1, f32[256]{0:T(256)S(1)} %add_rsqrt_fusion, s32[256]{0:T(256)S(1)} %multiply_add_fusion), kind=kOutput, calls=%fused_computation.4 | convolution fusion | flops 269877248 | bytes 2103296 | tf_op jit(solution)/shard_map/dot_general | solution.py:503
  49.4 0.0 copy-start
  49.4 59.3 %experts.1 = bf16[512,1024]{1,0:T(8,128)(2,1)} custom-call(bf16[512,1024]{1,0:T(8,128)(2,1)} %convolution_convert_fusion.1.buf_ref, bf16[1,1024,2816]{2,1,0:T(8,128)(2,1)} %w_in_hbm.1, bf16[1,2816,1024]{2,1,0:T(8,128)(2,1)} %w_back_hbm.1), custom_call_target="tpu_custom_call" | custom-call | tf_op jit(solution)/shard_map/experts/pallas_call | solution.py:440
  108.7 0.0 copy-done
  108.7 3.0 %fusion.1 = bf16[1,512,1024]{2,1,0:T(8,128)(2,1)} fusion(f32[256,1024]{1,0:T(8,128)S(1)} %get-tuple-element.12, bf16[512,1024]{1,0:T(8,128)(2,1)} %experts.1, bf16[1,512,1024]{2,1,0:T(8,128)(2,1)S(1)} %copy-done, pred[512]{0:T(512)(128)(4,1)S(1)} %fusion.9, s32[256]{0:T(256)S(1)} %multiply_add_fusion, s32[256]{0:T(256)S(1)} %bitcast.27), kind=kOutput, calls=%fused_computation.6 | convolution fusion | flops 538705920 | bytes 4196864 | tf_op jit(solution)/shard_map/dot_general | solution.py:509
  (2 shorter events, 0.0 us)
Async XLA Ops:
  0.0 47.9 %copy-start.1 = (f32[1024]{0:T(1024)S(1)}, f32[1024]{0:T(1024)}, u32[]{:S(2)}) copy-start(f32[1024]{0:T(1024)} %param.14) | copy-start | bytes 12292
  49.4 59.3 %copy-start = (bf16[1,512,1024]{2,1,0:T(8,128)(2,1)S(1)}, bf16[1,512,1024]{2,1,0:T(8,128)(2,1)}, u32[]{:S(2)}) copy-start(bf16[1,512,1024]{2,1,0:T(8,128)(2,1)} %param.11) | copy-start | bytes 3145732
